TPU v7x, 512 devices: a whole 4x8x8 slice. The times are simulated.
512 devices in a mesh: vocab: 64 (over x, y, core), tok: 8 (over z).
Axes of the slice: x: 4, y: 8, z: 8, core: 2. Of those that a mesh axis runs over, the one named last changes fastest.
Arguments:
- student_hidden: bfloat16 [256, 4608], P('vocab', 'tok'), may hold values from -6 to 6
- teacher_hidden: bfloat16 [256, 4608], P('vocab', 'tok'), may hold values from -6 to 6
- student_head: bfloat16 [128000, 4608], P('vocab', 'tok'), may hold values from -0.375 to 0.375
- teacher_head: bfloat16 [128000, 4608], P('vocab', 'tok'), may hold values from -0.375 to 0.375
- token_weight: float32 [256], replicated, may hold values from 2 to 32
Outputs:
- token_kl: float32 [256], P('tok')
- hidden_grad: float32 [256, 4608], P('vocab', 'tok')
All inputs are finite; a program needn't handle non-finite values.
Results may differ from a plain program's by a relative error of at most 0.0027.
Values may be sent and summed in bfloat16 or wider, within the bound.
A program may use at most 64 MiB of HBM per device.

v0:
```python
import jax
import jax.numpy as jnp
from jax import lax
from jax.sharding import PartitionSpec as P

softcap = 30.0


def sent_together(arrays, axis, dim, along):
    ends, at = ([], 0)
    for a in arrays[:-1]:
        at += a.shape[along]
        ends.append(at)
    both = jnp.concatenate(arrays, axis=along)
    return tuple(jnp.split(lax.all_gather(both, axis, axis=dim, tiled=True), ends, axis=along))


def copy_for_each(array, axis):
    length = lax.axis_size(axis)
    return lax.all_to_all(
        jnp.broadcast_to(array[None], (length, *array.shape)), axis, 0, 0, tiled=True
    )


def over_copies(array, axis):
    return copy_for_each(array, axis).sum(axis=0)


def in_one(arrays, axis):
    ends = [0]
    for a in arrays:
        ends.append(ends[-1] + a.size)
    subtotal = over_copies(jnp.concatenate([a.ravel() for a in arrays]), axis)
    return tuple((subtotal[b:e].reshape(a.shape) for a, b, e in zip(arrays, ends, ends[1:])))


def joined_along(pieces, dim):
    shape = list(pieces.shape[1:])
    shape[dim] *= pieces.shape[0]
    return jnp.moveaxis(pieces, 0, dim).reshape(shape)


def gather_directly(array, axis, dim):
    return joined_along(copy_for_each(array, axis), dim)


def in_blocks(array, dim, length):
    shape = array.shape
    pieces = array.reshape(*shape[:dim], length, shape[dim] // length, *shape[dim + 1 :])
    return jnp.moveaxis(pieces, dim, 0)


def sum_at_owner(array, axis, dim):
    pieces = in_blocks(array, dim, lax.axis_size(axis))
    arrived = lax.all_to_all(pieces, axis, split_axis=0, concat_axis=0, tiled=True)
    return arrived.sum(axis=0)


def per_device(student_hidden, teacher_hidden, student_head, teacher_head, token_weight):
    student_rows, teacher_rows = sent_together((student_hidden, teacher_hidden), "vocab", 0, 1)
    tokens_all = student_rows.shape[0]
    vocab_rows = student_head.shape[0]
    sub_rows = tokens_all // lax.axis_size("tok")
    part_student = jnp.einsum(
        "td,vd->tv", student_rows, student_head, preferred_element_type=jnp.float32
    )
    part_teacher = jnp.einsum(
        "td,vd->tv", teacher_rows, teacher_head, preferred_element_type=jnp.float32
    )
    summed = lax.psum_scatter(
        jnp.concatenate([part_student, part_teacher], axis=1),
        "tok",
        scatter_dimension=0,
        tiled=True,
    )
    weights = lax.dynamic_slice_in_dim(token_weight, lax.axis_index("tok") * sub_rows, sub_rows, 0)
    student_logits = softcap * jnp.tanh(summed[:, :vocab_rows] / softcap)
    teacher_logits = softcap * jnp.tanh(summed[:, vocab_rows:] / softcap)
    student_exp = jnp.exp(student_logits)
    teacher_exp = jnp.exp(teacher_logits)
    student_local = jnp.sum(student_exp, axis=1)
    teacher_local = jnp.sum(teacher_exp, axis=1)
    cross_local = jnp.sum(teacher_exp * (teacher_logits - student_logits), axis=1)
    student_total, teacher_total, cross = in_one(
        (student_local, teacher_local, cross_local), "vocab"
    )
    token_kl = cross / teacher_total - jnp.log(teacher_total) + jnp.log(student_total)
    slope = 1.0 - (student_logits / softcap) ** 2
    grad_logits = (
        weights[:, None]
        * (student_exp / student_total[:, None] - teacher_exp / teacher_total[:, None])
        * slope
    ).astype(jnp.bfloat16)
    grad_all = gather_directly(grad_logits, "tok", 0)
    hidden_grad = sum_at_owner(
        jnp.dot(grad_all, student_head, preferred_element_type=jnp.float32), "vocab", 0
    )
    return (token_kl, hidden_grad)


def solution(mesh):
    in_specs = (P("vocab", "tok"), P("vocab", "tok"), P("vocab", "tok"), P("vocab", "tok"), P())
    out_specs = (P("tok"), P("vocab", "tok"))
    return jax.shard_map(
        per_device, mesh=mesh, in_specs=in_specs, out_specs=out_specs, check_vma=False
    )
```

profile of v0, /device:TPU:1, one launch (start us, length us, event | category | flops | bytes accessed | tf_op | source)
XLA Modules:
  0.0 225.9 jit_solution(10667657736084343990)
XLA Ops:
  7.2 0.0 copy-start
  7.2 0.0 reduce-scatter.4.cloned.1.call-start
  7.2 0.9 maximum_bitcast_fusion
  8.2 53.9 %all-gather = bf16[64,4,1152]{2,1,0:T(4,128)(2,1)S(1)} all-gather(bf16[1,4,1152]{2,1,0:T(4,128)(2,1)S(1)} %maximum_bitcast_fusion), channel_id=1, replica_groups=mesh['vocab'=64,'tok'=8] {'vocab'}, dimensions={0}, use_global_device_ids=true | all-gather | bytes 599040 | tf_op jit(solution)/shard_map/all_gather | solution.py:15
  62.1 0.1 reshape.19
  62.2 3.0 %fusion.3 = f32[256,2000]{0,1:T(8,128)S(1)} fusion(bf16[2000,576]{0,1:T(8,128)(2,1)} %param.8, bf16[256,1152]{1,0:T(8,128)(2,1)S(1)} %reshape.19), kind=kOutput, calls=%fused_computation.4 | convolution fusion | flops 589824000 | bytes 4679680 | tf_op jit(solution)/shard_map/td,vd->tv/dot_general | solution.py:67
  65.2 0.0 copy-done
  65.3 1.2 fusion.5
  66.5 2.2 pad_maximum_fusion
  68.7 5.5 %copy.25 = f32[256,4000]{1,0:T(8,128)} copy(f32[256,4000]{0,1:T(8,128)} %pad_maximum_fusion) | data formatting | bytes 8192000
  74.2 0.0 copy-start.1
  74.2 0.0 reduce-scatter.4.cloned.1.call-update
  74.2 58.7 %reduce-scatter.4.cloned.1.call-done = f32[32,4000]{1,0:T(8,128)} async-done(((f32[256,4000]{1,0:T(8,128)}), f32[32,4000]{1,0:T(8,128)}) %reduce-scatter.4.cloned.1.call-update) | async-done | bytes 512016 | tf_op jit(solution)/shard_map/reduce_scatter | solution.py:70
  132.9 1.4 exponential_reduce_fusion
  134.3 0.1 pad_maximum_fusion.1
  134.3 0.6 broadcast_in_dim.4
  135.0 10.4 %all-to-all-start = ((f32[64,1,96]{2,1,0:T(1,128)}), f32[64,1,96]{2,1,0:T(1,128)S(1)}, u32[]{:S(2)}, u32[]{:S(2)}) async-start(f32[64,1,96]{2,1,0:T(1,128)} %broadcast_in_dim.4), calls=%async_computation | async-start | bytes 65536 | tf_op jit(solution)/shard_map/all_to_all | solution.py:20
  145.4 0.0 copy-done.1
  145.4 0.1 dynamic_slice.3
  145.5 9.2 %all-to-all-done = f32[64,1,96]{2,1,0:T(1,128)S(1)} async-done(((f32[64,1,96]{2,1,0:T(1,128)}), f32[64,1,96]{2,1,0:T(1,128)S(1)}, u32[]{:S(2)}, u32[]{:S(2)}) %all-to-all-start) | async-done | bytes 24608 | tf_op jit(solution)/shard_map/all_to_all | solution.py:20
  154.8 0.6 fusion.10
  155.4 1.2 multiply_convert_fusion
  156.6 0.1 broadcast_in_dim.5
  156.7 31.0 %all_to_all.16 = bf16[8,32,2000]{2,1,0:T(8,128)(2,1)S(1)} all-to-all(bf16[8,32,2000]{2,1,0:T(8,128)(2,1)S(1)} %broadcast_in_dim.5), channel_id=1, replica_groups=mesh['vocab'=64,'tok'=8] {'tok'}, dimensions={0} | all-to-all | bytes 2048000 | tf_op jit(solution)/shard_map/all_to_all | solution.py:20
  187.8 1.2 dot_general.13
  189.0 3.2 %fusion = f32[64,4,576]{2,0,1:T(8,128)S(1)} fusion(bf16[2000,576]{0,1:T(8,128)(2,1)S(1)} %copy-done, bf16[64,4,2000]{2,1,0:T(4,128)(2,1)} %dot_general.13), kind=kOutput, calls=%fused_computation.1 | convolution fusion | flops 589824000 | bytes 3917824 | tf_op jit(solution)/shard_map/dot_general | solution.py:96
  192.2 0.4 copy.24
  192.6 25.7 %all_to_all.17 = f32[64,4,576]{2,1,0:T(4,128)S(1)} all-to-all(f32[64,4,576]{2,1,0:T(4,128)S(1)} %copy.24), channel_id=1, replica_groups=mesh['vocab'=64,'tok'=8] {'vocab'}, dimensions={0} | all-to-all | bytes 1179648 | tf_op jit(solution)/shard_map/all_to_all | solution.py:55
  218.3 0.7 reduce_sum.49
  (1 shorter events, 0.0 us)
Async XLA Ops:
  7.2 58.1 %copy-start = (bf16[2000,576]{0,1:T(8,128)(2,1)S(1)}, bf16[2000,576]{0,1:T(8,128)(2,1)}, u32[]{:S(2)}) copy-start(bf16[2000,576]{0,1:T(8,128)(2,1)} %param.7) | copy-start | bytes 6912004
  7.2 125.7 %reduce-scatter.4.cloned.1.call-start = ((), (), s32[]{:S(2)}) async-start(), calls=%async_computation.4 | async-start | bytes 4718592 | tf_op jit(solution)/shard_map/reduce_scatter | solution.py:70
  74.2 71.3 %copy-start.1 = (f32[256]{0:T(256)S(1)}, f32[256]{0:T(256)}, u32[]{:S(2)}) copy-start(f32[256]{0:T(256)} %param.9) | copy-start | bytes 3076
  135.0 19.8 %all-to-all-start = ((f32[64,1,96]{2,1,0:T(1,128)}), f32[64,1,96]{2,1,0:T(1,128)S(1)}, u32[]{:S(2)}, u32[]{:S(2)}) async-start(f32[64,1,96]{2,1,0:T(1,128)} %broadcast_in_dim.4), calls=%async_computation | async-start | bytes 65536 | tf_op jit(solution)/shard_map/all_to_all | solution.py:20
Sparse Core Ops, SparseCore 0:
  74.3 58.5 reduce-scatter.3
where the time goes:
time: 226 us
  blocking collectives  111 us (49%)
  waiting for transfers between devices  68 us (30%)
  between operations  14.1 us (6%)
  starting transfers between devices  10.5 us (5%)
  local copies, waits for them, and re-layouts  8.1 us (4%)
  matrix products  7.43 us (3%)
  other arithmetic  7.16 us (3%)
    reduce_scatter x1, waiting for transfers between devices, per_device(): lax.psum_scatter(jnp.concatenate([part_student, part_teacher], axis=1), '...  58.7 us
    all_gather x1, blocking collectives, sent_together(): lax.all_gather(both, axis, axis=dim, tiled=True)  53.9 us
    all_to_all x1, blocking collectives, copy_for_each(): lax.all_to_all(jnp.broadcast_to(array[None], (length, *array.shape)), axi...  31 us
    all_to_all x1, blocking collectives, sum_at_owner(): lax.all_to_all(pieces, axis, split_axis=0, concat_axis=0, tiled=True)  25.7 us
    all_to_all x1, starting transfers between devices, copy_for_each(): lax.all_to_all(jnp.broadcast_to(array[None], (length, *array.shape)), axi...  10.4 us
    all_to_all x1, waiting for transfers between devices, copy_for_each(): lax.all_to_all(jnp.broadcast_to(array[None], (length, *array.shape)), axi...  9.22 us
    unnamed x6, local copies, waits for them, and re-layouts  5.65 us
  transfers between devices with their start and end apart: 2, of which 2 were waited for; matrix products, arithmetic and copies ran while one was open for 0% of the time, Pallas kernels for 0%

commit v1 on v0

v1 whole, which is shorter than its diff:
```python
import functools

import jax
import jax.numpy as jnp
from jax import lax
from jax.experimental import pallas as pl
from jax.experimental.pallas import tpu as pltpu
from jax.sharding import PartitionSpec as P

MESH = pl.DeviceIdType.MESH
f32, bf16 = jnp.float32, jnp.bfloat16
softcap = 30.0

def program(
    dims, sh_ref, th_ref, w_ref, sH_ref, tH_ref, kl_ref, hg_ref,
    H, hrecv, G, S, Pt, sbuf, rbuf, As, At, acc, st_own, st_in, gbuf, hgb, ecr, es, ey, exs, ex,
    hsem, a1s, a1r, a2r, a3r, a4r, a23s, a4s, bs, br, cs, cr, ds_, dr, ecs, ecrs, eys, eyr, exs_s, exr,
):
    X, Y, Z, VR, CH, NJ = dims
    V, L, Bc = 2 * X * Y, Z // 2, X * Y // Z
    R = 8 * Bc
    T = Z * R
    v, z = lax.axis_index("vocab"), lax.axis_index("tok")
    c, chip = lax.rem(v, 2), lax.div(v, 2)
    y, x = lax.rem(chip, Y), lax.div(chip, Y)

    def at(x_, y_, c_, z_=None):
        return {"vocab": (x_ * Y + y_) * 2 + c_, "tok": z if z_ is None else z_}

    def send(src, dst, ssem, rsem, dev):
        pltpu.make_async_remote_copy(
            src_ref=src, dst_ref=dst, send_sem=ssem, recv_sem=rsem, device_id=dev, device_id_type=MESH
        ).start()

    def await_bytes(ref, sem):
        pltpu.make_async_copy(ref, ref, sem).wait()

    partner = at(x, y, 1 - c)
    beside = [at(x, y, c, lax.rem(z + 1, Z)), at(x, y, c, lax.rem(z + Z - 1, Z))]
    sign = [1, -1]

    for m, ref in enumerate((sH_ref, tH_ref)):
        pltpu.make_async_copy(ref, H.at[m, pl.ds(0, VR)], hsem.at[m]).start()

    barrier = pltpu.get_barrier_semaphore()
    greeted = [partner, *beside]
    greeted += [at(x, lax.rem(y + d, Y), c) for d in range(1, Y)]
    greeted += [at(lax.rem(x + d, X), y, c) for d in range(1, X)]
    for dev in greeted:
        pl.semaphore_signal(barrier, inc=1, device_id=dev, device_id_type=MESH)
    if NJ * CH > VR:
        for m in range(2):
            H[m, VR:, :] = jnp.zeros((NJ * CH - VR, H.shape[2]), bf16)
    pl.semaphore_wait(barrier, len(greeted))

    for m, ref in enumerate((sh_ref, th_ref)):
        send(ref, hrecv.at[m], a1s.at[m], a1r.at[m], partner)
    for m in range(2):
        await_bytes(hrecv.at[m], a1r.at[m])

    def joined(ref, m):
        own, other = ref[...].astype(f32), hrecv[m].astype(f32)
        first, second = jnp.where(c == 0, own, other), jnp.where(c == 0, other, own)
        return jnp.concatenate([first, second], axis=0)

    G[c, chip] = jnp.where(c == 0, joined(sh_ref, 0), joined(th_ref, 1)).astype(bf16)
    far_first = sorted(range(1, Y), key=lambda d: -min(d, Y - d))
    for d in far_first:
        send(G.at[c, chip], G.at[c, chip], a23s, a2r.at[d - 1], at(x, lax.rem(y + d, Y), c))

    def along_x(slot):
        for d in range(1, X):
            send(G.at[c, slot], G.at[c, slot], a23s, a3r.at[d - 1], at(lax.rem(x + d, X), y, c))

    along_x(chip)
    for d in reversed(far_first):
        slot = x * Y + lax.rem(y + Y - d, Y)
        await_bytes(G.at[c, slot], a2r.at[d - 1])
        along_x(slot)
    for d in range(X):
        row = pl.ds(lax.rem(x + X - d, X) * Y, Y)
        if d:
            await_bytes(G.at[c, row], a3r.at[d - 1])
        send(G.at[c, row], G.at[c, row], a4s, a4r.at[d], partner)
    for d in range(X):
        row = pl.ds(lax.rem(x + X - d, X) * Y, Y)
        await_bytes(G.at[1 - c, row], a4r.at[d])

    top = lax.broadcasted_iota(jnp.int32, (8, G.shape[3]), 0) < 4
    for m in range(2):

        def arrange(b, carry, m=m):
            for p in range(Bc // 2):
                a, o = G[m, b * Bc + 2 * p].astype(f32), G[m, b * Bc + 2 * p + 1].astype(f32)
                a4, o4 = pltpu.roll(a, 4, 0), pltpu.roll(o, 4, 0)
                S[m, b, p] = jnp.where(top, a, o4).astype(bf16)
                S[m, b, Bc // 2 + p] = jnp.where(top, a4, o).astype(bf16)
            return carry

        lax.fori_loop(0, Z, arrange, 0)

    for m in range(2):
        await_bytes(H.at[m, pl.ds(0, VR)], hsem.at[m])

    for k in range(L, 0, -1):

        def stage(j, carry, k=k):
            if k == L:
                for m in range(2):
                    rows = S[m].astype(f32).reshape(T, S.shape[4]).astype(bf16)
                    cols = H[m, pl.ds(pl.multiple_of(j * CH, CH), CH), :]
                    Pt[j, m] = lax.dot_general(
                        rows, cols, (((1,), (1,)), ((), ())), preferred_element_type=f32
                    )
            for m in range(2):
                for s in range(2):
                    first = L if s == m else L - 1
                    if k > first:
                        continue
                    dest = lax.rem(z + sign[s] * k + Z, Z)
                    part = Pt[j, m, pl.ds(pl.multiple_of(dest * R, R), R), :]
                    if k < first:
                        await_bytes(rbuf.at[s, k, j, m], br.at[s, k, j, m])
                        part = part + rbuf[s, k, j, m]
                    if k == L:
                        slot = j * 2 + m
                    else:
                        slot = 2 * NJ + ((L - 1 - k) * 2 + s) * 2 * NJ + j * 2 + m
                    sbuf[slot] = part
                    send(sbuf.at[slot], rbuf.at[s, k - 1, j, m], bs, br.at[s, k - 1, j, m], beside[s])
            return carry

        lax.fori_loop(0, NJ, stage, 0)

    acc[...] = jnp.zeros(acc.shape, f32)

    def finish(j, carry):
        logits = []
        for m in range(2):
            raw = Pt[j, m, pl.ds(pl.multiple_of(z * R, R), R), :]
            for s in range(2):
                await_bytes(rbuf.at[s, 0, j, m], br.at[s, 0, j, m])
                raw = raw + rbuf[s, 0, j, m]
            logits.append(jnp.tanh(raw * (1.0 / softcap)))
        held = lax.broadcasted_iota(jnp.int32, (R, CH), 1) + j * CH < VR
        slope = 1.0 - logits[0] * logits[0]
        sl, tl = softcap * logits[0], softcap * logits[1]
        se, te = jnp.where(held, jnp.exp(sl), 0.0), jnp.where(held, jnp.exp(tl), 0.0)
        As[j], At[j] = se * slope, te * slope
        for n, value in enumerate((se, te, te * (tl - sl))):
            acc[n] += functools.reduce(jnp.add, [value[:, i : i + 128] for i in range(0, CH, 128)])
        return carry

    lax.fori_loop(0, NJ, finish, 0)

    lane = lax.broadcasted_iota(jnp.int32, (R, 128), 1)
    row = lax.broadcasted_iota(jnp.int32, (R, 128), 0)
    packed = jnp.zeros((R, 128), f32)
    for n in range(3):
        packed += jnp.where(lane == row + n * R, jnp.sum(acc[n], axis=1, keepdims=True), 0.0)
    mine = jnp.sum(packed, axis=0, keepdims=True)
    st_own[...] = mine
    st_in[v] = mine

    def tell(d, carry):
        send(st_own, st_in.at[v], cs, cr, {"vocab": lax.rem(v + d, V), "tok": z})
        return carry

    lax.fori_loop(1, V, tell, 0)
    await_bytes(st_in.at[pl.ds(0, V - 1)], cr)
    total = jnp.sum(st_in[...], axis=0)
    spread = [jnp.sum(jnp.where(lane == row + n * R, total, 0.0), axis=1, keepdims=True) for n in range(3)]
    student_total, teacher_total, cross = spread

    def natural(r):
        half = R // 2
        in_core = lax.rem(r, half)
        return lax.div(in_core, 4) * 8 + lax.div(r, half) * 4 + lax.rem(in_core, 4)

    wlane = lax.broadcasted_iota(jnp.int32, (R, T), 1)
    wrow = lax.broadcasted_iota(jnp.int32, (R, T), 0)
    weight = jnp.sum(jnp.where(wlane == z * R + natural(wrow), w_ref[...], 0.0), axis=1, keepdims=True)
    student_scale, teacher_scale = weight / student_total, weight / teacher_total

    for j in range(NJ):
        gbuf[z, j] = (As[j] * student_scale - At[j] * teacher_scale).astype(bf16)
        for s in range(2):
            send(gbuf.at[z, j], gbuf.at[z, j], ds_, dr.at[s, 0, j], beside[s])

    kl = cross / teacher_total - jnp.log(teacher_total) + jnp.log(student_total)
    kl_row = jnp.sum(jnp.where(lane == natural(row), kl, 0.0), axis=0, keepdims=True)
    kl_ref[...] = kl_row[:, :R]

    half = R // 2
    blocks_in_x = Y // Bc

    def to_partner(slots, sources):
        total_ = None
        for j in range(NJ):
            rows = jnp.concatenate([gbuf[t, j] for t in sources], axis=0) if len(sources) > 1 else gbuf[sources[0], j]
            part = jnp.dot(rows, H[0, j * CH : (j + 1) * CH, :], preferred_element_type=f32)
            total_ = part if total_ is None else total_ + part
        for n, slot in enumerate(slots):
            hgb[slot] = total_[n * R : (n + 1) * R]
            theirs = pl.ds(pl.multiple_of((1 - c) * half, half), half)
            send(hgb.at[slot, theirs], ecr.at[slot], ecs, ecrs.at[slot], partner)

    def along_y(slots, sources):
        for slot, t in zip(slots, sources):
            await_bytes(ecr.at[slot], ecrs.at[slot])
            ours = pl.ds(pl.multiple_of(c * half, half), half)
            both = hgb[slot, ours] + ecr[slot]
            tx, ty = lax.div(t, blocks_in_x), lax.rem(t, blocks_in_x) * Bc
            for i in range(Bc):
                piece = both[4 * i : 4 * i + 4]
                es[slot, i] = piece

                @pl.when(ty + i == y)
                def _():
                    ey[tx * Y + y] = piece

                @pl.when(ty + i != y)
                def _():
                    send(es.at[slot, i], ey.at[tx * Y + y], eys, eyr.at[tx], at(x, ty + i, c))

    pending = ([0], [z])
    to_partner(*pending)
    for d in range(1, L + 1):
        for j in range(NJ):
            for s in range(2):
                reach = L if s == j % 2 else L - 1
                if d > reach:
                    continue
                src = lax.rem(z - sign[s] * d + Z, Z)
                await_bytes(gbuf.at[src, j], dr.at[s, d - 1, j])
                if d < reach:
                    send(gbuf.at[src, j], gbuf.at[src, j], ds_, dr.at[s, d, j], beside[s])
        if d < L:
            now = ([2 * d - 1, 2 * d], [lax.rem(z - d + Z, Z), lax.rem(z + d, Z)])
        else:
            now = ([2 * d - 1], [lax.rem(z + d, Z)])
        to_partner(*now)
        along_y(*pending)
        pending = now
    along_y(*pending)

    last = lax.div(lax.rem(z + L, Z), blocks_in_x)
    for i in range(X):
        tx = lax.rem(last + 1 + i, X)
        await_bytes(ey.at[pl.ds(0, Y - 1)], eyr.at[tx])
        summed = jnp.sum(ey[pl.ds(tx * Y, Y)], axis=0)
        exs[tx] = summed

        @pl.when(tx == x)
        def _():
            ex[x] = summed

        @pl.when(tx != x)
        def _():
            send(exs.at[tx], ex.at[x], exs_s, exr, at(tx, y, c))

    await_bytes(ex.at[pl.ds(0, X - 1)], exr)
    hg_ref[...] = jnp.sum(ex[...], axis=0)

    for m in range(2):
        await_bytes(hrecv.at[m], a1s.at[m])
    await_bytes(G.at[0, pl.ds(0, X * Y - 1)], a23s)
    await_bytes(G.at[0], a4s)
    await_bytes(sbuf, bs)
    await_bytes(st_in.at[pl.ds(0, V - 1)], cs)
    await_bytes(gbuf.at[pl.ds(0, Z - 1)], ds_)
    await_bytes(ecr, ecs)
    await_bytes(ey.at[pl.ds(0, X * (Y - 1))], eys)
    await_bytes(ex.at[pl.ds(0, X - 1)], exs_s)


def build(mesh, X, Y, Z, CH):
    V, L, Bc = 2 * X * Y, Z // 2, X * Y // Z
    R = 8 * Bc

    def per_device(student_hidden, teacher_hidden, student_head, teacher_head, token_weight):
        VR, K = student_head.shape
        NJ = -(-VR // CH)
        T = token_weight.shape[0]
        dma = pltpu.SemaphoreType.DMA
        vmem = pl.BlockSpec(memory_space=pltpu.VMEM)
        hbm = pl.BlockSpec(memory_space=pl.ANY)
        kl, hg = pl.pallas_call(
            functools.partial(program, (X, Y, Z, VR, CH, NJ)),
            out_shape=(jax.ShapeDtypeStruct((1, R), f32), jax.ShapeDtypeStruct((4, K), f32)),
            in_specs=[vmem, vmem, vmem, hbm, hbm],
            out_specs=(vmem, vmem),
            scratch_shapes=[
                pltpu.VMEM((2, NJ * CH, K), bf16),
                pltpu.VMEM((2, 4, K), bf16),
                pltpu.VMEM((2, X * Y, 8, K), bf16),
                pltpu.VMEM((2, Z, Bc, 8, K), bf16),
                pltpu.VMEM((NJ, 2, T, CH), f32),
                pltpu.VMEM((2 * NJ * (2 * L - 1), R, CH), f32),
                pltpu.VMEM((2, L, NJ, 2, R, CH), f32),
                pltpu.VMEM((NJ, R, CH), f32),
                pltpu.VMEM((NJ, R, CH), f32),
                pltpu.VMEM((3, R, 128), f32),
                pltpu.VMEM((1, 128), f32),
                pltpu.VMEM((V, 1, 128), f32),
                pltpu.VMEM((Z, NJ, R, CH), bf16),
                pltpu.VMEM((Z, R, K), f32),
                pltpu.VMEM((Z, R // 2, K), f32),
                pltpu.VMEM((Z, Bc, 4, K), f32),
                pltpu.VMEM((X * Y, 4, K), f32),
                pltpu.VMEM((X, 4, K), f32),
                pltpu.VMEM((X, 4, K), f32),
                dma((2,)),
                dma((2,)),
                dma((2,)),
                dma((Y - 1,)),
                dma((X - 1,)),
                dma((X,)),
                dma,
                dma,
                dma,
                dma((2, L, NJ, 2)),
                dma,
                dma,
                dma,
                dma((2, L, NJ)),
                dma,
                dma((Z,)),
                dma,
                dma((X,)),
                dma,
                dma,
            ],
            compiler_params=pltpu.CompilerParams(
                collective_id=0, has_side_effects=True, vmem_limit_bytes=56 * 1024 * 1024
            ),
        )(student_hidden, teacher_hidden, token_weight.reshape(1, T), student_head, teacher_head)
        return kl.reshape(R), hg

    in_specs = (P("vocab", "tok"), P("vocab", "tok"), P("vocab", "tok"), P("vocab", "tok"), P())
    return jax.shard_map(
        per_device, mesh=mesh, in_specs=in_specs, out_specs=(P("tok"), P("vocab", "tok")), check_vma=False
    )


def solution(mesh):
    return build(mesh, 4, 8, 8, 512)
```

time: 226 us -> 112 us (0.50)
  blocking collectives: 111 us -> 0 us
  Pallas kernels: 0 us -> 99.9 us
  waiting for transfers between devices: 68 us -> 0 us
  between operations: 14.1 us -> 0.65 us
  starting transfers between devices: 10.5 us -> 0 us
  matrix products: 7.43 us -> 0 us
  other arithmetic: 7.16 us -> 0 us
    pallas_call x0 -> x1, Pallas kernels: none -> 99.9 us  [per_device(): pl.pallas_call(functools.partial(program, (X, Y, Z, VR, CH, NJ)), out_sha...]
    reduce_scatter x1 -> x0, waiting for transfers between devices: 58.7 us -> none  [per_device(): lax.psum_scatter(jnp.concatenate([part_student, part_teacher], axis=1), '...]
    all_to_all x2 -> x0, blocking collectives: 56.7 us -> none  [the longest x1 31 us: copy_for_each(): lax.all_to_all(jnp.broadcast_to(array[None], (length, *array.shape)), axi...]
    all_gather x1 -> x0, blocking collectives: 53.9 us -> none  [sent_together(): lax.all_gather(both, axis, axis=dim, tiled=True)]
    all_to_all x1 -> x0, starting transfers between devices: 10.4 us -> none  [copy_for_each(): lax.all_to_all(jnp.broadcast_to(array[None], (length, *array.shape)), axi...]
    all_to_all x1 -> x0, waiting for transfers between devices: 9.22 us -> none  [copy_for_each(): lax.all_to_all(jnp.broadcast_to(array[None], (length, *array.shape)), axi...]
    dot_general x3 -> x0, matrix products: 7.43 us -> none  [the longest x1 3.19 us: per_device(): jnp.dot(grad_all, student_head, preferred_element_type=jnp.float32)]
    unnamed x6, local copies, waits for them, and re-layouts: 5.65 us -> 9.51 us
  transfers between devices with their start and end apart: 2 -> 0, of which waited for: 2 -> 0; matrix products, arithmetic and copies ran while one was open for 0% -> 0% of each run, Pallas kernels for 0% -> 0%
where the time goes in v1:
time: 112 us; the launch traced here: 110 us
  Pallas kernels  99.9 us (89%)
  local copies, waits for them, and re-layouts  9.51 us (8%)
    pallas_call x1, Pallas kernels, per_device(): pl.pallas_call(functools.partial(program, (X, Y, Z, VR, CH, NJ)), out_sha...  99.9 us
    unnamed x6, local copies, waits for them, and re-layouts  9.51 us

profile of v1, /device:TPU:1, one launch (start us, length us, event | category | flops | bytes accessed | tf_op | source)
XLA Modules:
  0.0 110.0 jit_solution(16400943507516734596)
XLA Ops:
  0.6 0.0 copy-start
  0.6 4.5 %copy.7.sH_ref = bf16[2000,576]{1,0:T(8,128)(2,1)} copy(bf16[2000,576]{0,1:T(8,128)(2,1)} %param.7) | data formatting | bytes 4608000 | tf_op args[2]
  5.1 0.0 copy-done
  5.1 2.6 %copy.8.tH_ref = bf16[2000,576]{1,0:T(8,128)(2,1)} copy(bf16[2000,576]{0,1:T(8,128)(2,1)S(1)} %copy-done) | data formatting | bytes 4608000 | tf_op args[3]
  7.7 99.9 %shard_map.68 = (f32[1,32]{1,0:T(1,128)}, f32[4,576]{1,0:T(4,128)}) custom-call(bf16[4,576]{1,0:T(4,128)(2,1)} %sh_ref.1, bf16[4,576]{1,0:T(4,128)(2,1)} %th_ref.1, f32[1,256]{1,0:T(1,128)} %bitcast.2, bf16[2000,576]{1,0:T(8,128)(2,1)} %copy.7.sH_ref, bf16[2000,576]{1,0:T(8,128)(2,1)} %copy.8.tH_ref), custom_call_target="tpu_custom_call" | custom-call | tf_op jit(solution)/shard_map/pallas_call | solution.py:288
  107.6 1.2 %copy.11 = f32[32]{0:T(128)} copy(f32[32]{0:T(128)} %bitcast.3) | data formatting | bytes 256
  108.7 1.3 %copy.12 = f32[4,576]{1,0:T(4,128)} copy(f32[4,576]{1,0:T(4,128)} %get-tuple-element.9) | data formatting | bytes 18432
Async XLA Ops:
  0.6 4.5 %copy-start = (bf16[2000,576]{0,1:T(8,128)(2,1)S(1)}, bf16[2000,576]{0,1:T(8,128)(2,1)}, u32[]{:S(2)}) copy-start(bf16[2000,576]{0,1:T(8,128)(2,1)} %param.8) | copy-start | bytes 6912004

commit v2 on v1

--- a/solution.py
+++ b/solution.py
@@ -13,8 +13,8 @@
 
 def program(
     dims, sh_ref, th_ref, w_ref, sH_ref, tH_ref, kl_ref, hg_ref,
-    H, hrecv, G, S, Pt, sbuf, rbuf, As, At, acc, st_own, st_in, gbuf, hgb, ecr, es, ey, exs, ex,
-    hsem, a1s, a1r, a2r, a3r, a4r, a23s, a4s, bs, br, cs, cr, ds_, dr, ecs, ecrs, eys, eyr, exs_s, exr,
+    H, G, S, Pt, sbuf, rbuf, As, At, acc, st_own, st_in, gbuf, hgb, ecr, es, ey, exs, ex,
+    hsem, a2r, a3r, a4r, a23s, a4s, bs, br, cs, cr, ds_, dr, ecs, ecrs, eys, eyr, exs_s, exr,
 ):
     X, Y, Z, VR, CH, NJ = dims
     V, L, Bc = 2 * X * Y, Z // 2, X * Y // Z
@@ -40,7 +40,12 @@
     sign = [1, -1]
 
     for m, ref in enumerate((sH_ref, tH_ref)):
-        pltpu.make_async_copy(ref, H.at[m, pl.ds(0, VR)], hsem.at[m]).start()
+        pltpu.make_async_copy(ref, H.at[m], hsem.at[m]).start()
+    for m, ref in enumerate((sh_ref, th_ref)):
+        G[c, chip, m] = ref[...]
+    if NJ * CH > VR:
+        for m in range(2):
+            Pt[NJ - 1, m, :, CH - 128 :] = jnp.zeros((T, 128), f32)
 
     barrier = pltpu.get_barrier_semaphore()
     greeted = [partner, *beside]
@@ -48,22 +53,8 @@
     greeted += [at(lax.rem(x + d, X), y, c) for d in range(1, X)]
     for dev in greeted:
         pl.semaphore_signal(barrier, inc=1, device_id=dev, device_id_type=MESH)
-    if NJ * CH > VR:
-        for m in range(2):
-            H[m, VR:, :] = jnp.zeros((NJ * CH - VR, H.shape[2]), bf16)
     pl.semaphore_wait(barrier, len(greeted))
 
-    for m, ref in enumerate((sh_ref, th_ref)):
-        send(ref, hrecv.at[m], a1s.at[m], a1r.at[m], partner)
-    for m in range(2):
-        await_bytes(hrecv.at[m], a1r.at[m])
-
-    def joined(ref, m):
-        own, other = ref[...].astype(f32), hrecv[m].astype(f32)
-        first, second = jnp.where(c == 0, own, other), jnp.where(c == 0, other, own)
-        return jnp.concatenate([first, second], axis=0)
-
-    G[c, chip] = jnp.where(c == 0, joined(sh_ref, 0), joined(th_ref, 1)).astype(bf16)
     far_first = sorted(range(1, Y), key=lambda d: -min(d, Y - d))
     for d in far_first:
         send(G.at[c, chip], G.at[c, chip], a23s, a2r.at[d - 1], at(x, lax.rem(y + d, Y), c))
@@ -86,32 +77,29 @@
         row = pl.ds(lax.rem(x + X - d, X) * Y, Y)
         await_bytes(G.at[1 - c, row], a4r.at[d])
 
-    top = lax.broadcasted_iota(jnp.int32, (8, G.shape[3]), 0) < 4
+    half = R // 2
     for m in range(2):
-
-        def arrange(b, carry, m=m):
-            for p in range(Bc // 2):
-                a, o = G[m, b * Bc + 2 * p].astype(f32), G[m, b * Bc + 2 * p + 1].astype(f32)
-                a4, o4 = pltpu.roll(a, 4, 0), pltpu.roll(o, 4, 0)
-                S[m, b, p] = jnp.where(top, a, o4).astype(bf16)
-                S[m, b, Bc // 2 + p] = jnp.where(top, a4, o).astype(bf16)
-            return carry
-
-        lax.fori_loop(0, Z, arrange, 0)
+        for core in range(2):
+
+            def arrange(b, carry, m=m, core=core):
+                rows = [G[core, b * Bc + p, m].astype(f32) for p in range(Bc)]
+                place = pl.ds(pl.multiple_of(b * R + core * half, half), half)
+                S[m, place, :] = jnp.concatenate(rows, axis=0).astype(bf16)
+                return carry
+
+            lax.fori_loop(0, Z, arrange, 0)
 
     for m in range(2):
-        await_bytes(H.at[m, pl.ds(0, VR)], hsem.at[m])
+        await_bytes(H.at[m], hsem.at[m])
 
     for k in range(L, 0, -1):
 
         def stage(j, carry, k=k):
             if k == L:
+                width = min(CH, VR - j * CH)
                 for m in range(2):
-                    rows = S[m].astype(f32).reshape(T, S.shape[4]).astype(bf16)
-                    cols = H[m, pl.ds(pl.multiple_of(j * CH, CH), CH), :]
-                    Pt[j, m] = lax.dot_general(
-                        rows, cols, (((1,), (1,)), ((), ())), preferred_element_type=f32
-                    )
+                    cols = H[m, :, j * CH : j * CH + width]
+                    Pt[j, m, :, :width] = jnp.dot(S[m], cols, preferred_element_type=f32)
             for m in range(2):
                 for s in range(2):
                     first = L if s == m else L - 1
@@ -130,7 +118,11 @@
                     send(sbuf.at[slot], rbuf.at[s, k - 1, j, m], bs, br.at[s, k - 1, j, m], beside[s])
             return carry
 
-        lax.fori_loop(0, NJ, stage, 0)
+        if k == L:
+            for j in range(NJ):
+                stage(j, 0)
+        else:
+            lax.fori_loop(0, NJ, stage, 0)
 
     acc[...] = jnp.zeros(acc.shape, f32)
 
@@ -191,14 +183,19 @@
     kl_row = jnp.sum(jnp.where(lane == natural(row), kl, 0.0), axis=0, keepdims=True)
     kl_ref[...] = kl_row[:, :R]
 
-    half = R // 2
     blocks_in_x = Y // Bc
 
     def to_partner(slots, sources):
         total_ = None
         for j in range(NJ):
+            width = min(CH, VR - j * CH)
             rows = jnp.concatenate([gbuf[t, j] for t in sources], axis=0) if len(sources) > 1 else gbuf[sources[0], j]
-            part = jnp.dot(rows, H[0, j * CH : (j + 1) * CH, :], preferred_element_type=f32)
+            part = lax.dot_general(
+                rows[:, :width],
+                H[0, :, j * CH : j * CH + width],
+                (((1,), (1,)), ((), ())),
+                preferred_element_type=f32,
+            )
             total_ = part if total_ is None else total_ + part
         for n, slot in enumerate(slots):
             hgb[slot] = total_[n * R : (n + 1) * R]
@@ -262,8 +259,6 @@
     await_bytes(ex.at[pl.ds(0, X - 1)], exr)
     hg_ref[...] = jnp.sum(ex[...], axis=0)
 
-    for m in range(2):
-        await_bytes(hrecv.at[m], a1s.at[m])
     await_bytes(G.at[0, pl.ds(0, X * Y - 1)], a23s)
     await_bytes(G.at[0], a4s)
     await_bytes(sbuf, bs)
@@ -274,12 +269,17 @@
     await_bytes(ex.at[pl.ds(0, X - 1)], exs_s)
 
 
+def hand_out(kl_ref, hg_ref, kl_out, hg_out):
+    kl_out[...] = kl_ref[...]
+    hg_out[...] = hg_ref[...]
+
+
 def build(mesh, X, Y, Z, CH):
     V, L, Bc = 2 * X * Y, Z // 2, X * Y // Z
     R = 8 * Bc
 
     def per_device(student_hidden, teacher_hidden, student_head, teacher_head, token_weight):
-        VR, K = student_head.shape
+        K, VR = student_head.shape[1], student_head.shape[0]
         NJ = -(-VR // CH)
         T = token_weight.shape[0]
         dma = pltpu.SemaphoreType.DMA
@@ -291,10 +291,9 @@
             in_specs=[vmem, vmem, vmem, hbm, hbm],
             out_specs=(vmem, vmem),
             scratch_shapes=[
-                pltpu.VMEM((2, NJ * CH, K), bf16),
-                pltpu.VMEM((2, 4, K), bf16),
-                pltpu.VMEM((2, X * Y, 8, K), bf16),
-                pltpu.VMEM((2, Z, Bc, 8, K), bf16),
+                pltpu.VMEM((2, K, VR), bf16),
+                pltpu.VMEM((2, X * Y, 2, 4, K), bf16),
+                pltpu.VMEM((2, T, K), bf16),
                 pltpu.VMEM((NJ, 2, T, CH), f32),
                 pltpu.VMEM((2 * NJ * (2 * L - 1), R, CH), f32),
                 pltpu.VMEM((2, L, NJ, 2, R, CH), f32),
@@ -311,8 +310,6 @@
                 pltpu.VMEM((X, 4, K), f32),
                 pltpu.VMEM((X, 4, K), f32),
                 dma((2,)),
-                dma((2,)),
-                dma((2,)),
                 dma((Y - 1,)),
                 dma((X - 1,)),
                 dma((X,)),
@@ -334,7 +331,13 @@
             compiler_params=pltpu.CompilerParams(
                 collective_id=0, has_side_effects=True, vmem_limit_bytes=56 * 1024 * 1024
             ),
-        )(student_hidden, teacher_hidden, token_weight.reshape(1, T), student_head, teacher_head)
+        )(student_hidden, teacher_hidden, token_weight.reshape(1, T), student_head.T, teacher_head.T)
+        kl, hg = pl.pallas_call(
+            hand_out,
+            out_shape=(jax.ShapeDtypeStruct((1, R), f32), jax.ShapeDtypeStruct((4, K), f32)),
+            in_specs=[vmem, vmem],
+            out_specs=(vmem, vmem),
+        )(kl, hg)
         return kl.reshape(R), hg
 
     in_specs = (P("vocab", "tok"), P("vocab", "tok"), P("vocab", "tok"), P("vocab", "tok"), P())

time: 112 us -> 101 us (0.902)
  local copies, waits for them, and re-layouts: 9.51 us -> 0 us
    unnamed x6 -> x0, local copies, waits for them, and re-layouts: 9.51 us -> none
    pallas_call x1, Pallas kernels: 99.9 us -> 97.8 us  [per_device(): pl.pallas_call(functools.partial(program, (X, Y, Z, VR, CH, NJ)), out_sha...]
    pallas_call x0 -> x1, Pallas kernels: none -> 1.31 us  [per_device(): pl.pallas_call(hand_out, out_shape=(jax.ShapeDtypeStruct((1, R), f32), ja...]
where the time goes in v2:
time: 101 us; the launch traced here: 99.7 us
  Pallas kernels  99.1 us (98%)
    pallas_call x1, Pallas kernels, per_device(): pl.pallas_call(functools.partial(program, (X, Y, Z, VR, CH, NJ)), out_sha...  97.8 us

profile of v2, /device:TPU:1, one launch (start us, length us, event | category | flops | bytes accessed | tf_op | source)
XLA Modules:
  0.0 99.7 jit_solution(4352602742806529308)
XLA Ops:
  0.6 97.8 %shard_map.68 = (f32[1,32]{1,0:T(1,128)}, f32[4,576]{1,0:T(4,128)}) custom-call(bf16[4,576]{1,0:T(4,128)(2,1)} %sh_ref.1, bf16[4,576]{1,0:T(4,128)(2,1)} %th_ref.1, f32[1,256]{1,0:T(1,128)} %bitcast.6, bf16[576,2000]{1,0:T(8,128)(2,1)} %bitcast.4, bf16[576,2000]{1,0:T(8,128)(2,1)} %bitcast.5), custom_call_target="tpu_custom_call" | custom-call | tf_op jit(solution)/shard_map/pallas_call | solution.py:288
  98.4 1.3 %shard_map.69 = (f32[1,32]{1,0:T(1,128)}, f32[4,576]{1,0:T(4,128)}) custom-call(f32[1,32]{1,0:T(1,128)} %get-tuple-element.6.kl_ref, f32[4,576]{1,0:T(4,128)} %get-tuple-element.7.hg_ref), custom_call_target="tpu_custom_call" | custom-call | tf_op jit(solution)/shard_map/pallas_call | solution.py:335

commit v3 on v2

--- a/solution.py
+++ b/solution.py
@@ -10,6 +10,39 @@
 MESH = pl.DeviceIdType.MESH
 f32, bf16 = jnp.float32, jnp.bfloat16
 softcap = 30.0
+
+BEND = 24.0
+EDGE, ROOM = 1.01, 0.97
+BASE = 251
+MOST = float(BASE**3 // 2)
+
+
+def power(e):
+    return jnp.exp2(e).astype(bf16).astype(f32)
+
+
+def encode(s):
+    n = s.shape[1] // 4
+    u = s / (jnp.abs(s) + BEND)
+    whole = jnp.floor(u[:, 3 * n :] * MOST + 0.5)
+    high = jnp.floor(whole * (1.0 / BASE**2) + 0.5)
+    rest = whole - high * float(BASE**2)
+    middle = jnp.floor(rest * (1.0 / BASE) + 0.5)
+    low = rest - middle * float(BASE)
+    fill = u[:, : 3 * n] * ROOM
+    words = jnp.where(fill < 0, fill - EDGE, fill + EDGE)
+    return [words[:, i * n : (i + 1) * n] * power(e) for i, e in enumerate((high, middle, low))]
+
+
+def decode(words):
+    n = words.shape[1] // 3
+    size = jnp.abs(words)
+    e = jnp.floor(jnp.log2(size))
+    fill = size * power(-e) - EDGE
+    a = fill / (ROOM - fill) * BEND
+    first = jnp.where(words < 0, -a, a)
+    u = (e[:, :n] * float(BASE**2) + e[:, n : 2 * n] * float(BASE) + e[:, 2 * n :]) * (1.0 / MOST)
+    return jnp.concatenate([first, u / (1.0 - jnp.abs(u)) * BEND], axis=1)
 
 def program(
     dims, sh_ref, th_ref, w_ref, sH_ref, tH_ref, kl_ref, hg_ref,
@@ -109,12 +142,13 @@
                     part = Pt[j, m, pl.ds(pl.multiple_of(dest * R, R), R), :]
                     if k < first:
                         await_bytes(rbuf.at[s, k, j, m], br.at[s, k, j, m])
-                        part = part + rbuf[s, k, j, m]
+                        part = part + decode(rbuf[s, k, j, m])
                     if k == L:
                         slot = j * 2 + m
                     else:
                         slot = 2 * NJ + ((L - 1 - k) * 2 + s) * 2 * NJ + j * 2 + m
-                    sbuf[slot] = part
+                    for i, word in enumerate(encode(part)):
+                        sbuf[slot, :, i * CH // 4 : (i + 1) * CH // 4] = word
                     send(sbuf.at[slot], rbuf.at[s, k - 1, j, m], bs, br.at[s, k - 1, j, m], beside[s])
             return carry
 
@@ -132,7 +166,7 @@
             raw = Pt[j, m, pl.ds(pl.multiple_of(z * R, R), R), :]
             for s in range(2):
                 await_bytes(rbuf.at[s, 0, j, m], br.at[s, 0, j, m])
-                raw = raw + rbuf[s, 0, j, m]
+                raw = raw + decode(rbuf[s, 0, j, m])
             logits.append(jnp.tanh(raw * (1.0 / softcap)))
         held = lax.broadcasted_iota(jnp.int32, (R, CH), 1) + j * CH < VR
         slope = 1.0 - logits[0] * logits[0]
@@ -295,8 +329,8 @@
                 pltpu.VMEM((2, X * Y, 2, 4, K), bf16),
                 pltpu.VMEM((2, T, K), bf16),
                 pltpu.VMEM((NJ, 2, T, CH), f32),
-                pltpu.VMEM((2 * NJ * (2 * L - 1), R, CH), f32),
-                pltpu.VMEM((2, L, NJ, 2, R, CH), f32),
+                pltpu.VMEM((2 * NJ * (2 * L - 1), R, 3 * CH // 4), f32),
+                pltpu.VMEM((2, L, NJ, 2, R, 3 * CH // 4), f32),
                 pltpu.VMEM((NJ, R, CH), f32),
                 pltpu.VMEM((NJ, R, CH), f32),
                 pltpu.VMEM((3, R, 128), f32),

time: 101 us -> 91.5 us (0.906)
  Pallas kernels: 99.1 us -> 89.4 us
    pallas_call x1, Pallas kernels: 97.8 us -> 88 us  [per_device(): pl.pallas_call(functools.partial(program, (X, Y, Z, VR, CH, NJ)), out_sha...]
where the time goes in v3:
time: 91.5 us; the launch traced here: 90 us
  Pallas kernels  89.4 us (98%)
    pallas_call x1, Pallas kernels, per_device(): pl.pallas_call(functools.partial(program, (X, Y, Z, VR, CH, NJ)), out_sha...  88 us

profile of v3, /device:TPU:1, one launch (start us, length us, event | category | flops | bytes accessed | tf_op | source)
XLA Modules:
  0.0 90.0 jit_solution(1115758149826725004)
XLA Ops:
  0.6 88.0 %shard_map.68 = (f32[1,32]{1,0:T(1,128)}, f32[4,576]{1,0:T(4,128)}) custom-call(bf16[4,576]{1,0:T(4,128)(2,1)} %sh_ref.1, bf16[4,576]{1,0:T(4,128)(2,1)} %th_ref.1, f32[1,256]{1,0:T(1,128)} %bitcast.6, bf16[576,2000]{1,0:T(8,128)(2,1)} %bitcast.4, bf16[576,2000]{1,0:T(8,128)(2,1)} %bitcast.5), custom_call_target="tpu_custom_call" | custom-call | tf_op jit(solution)/shard_map/pallas_call | solution.py:322
  88.7 1.3 %shard_map.69 = (f32[1,32]{1,0:T(1,128)}, f32[4,576]{1,0:T(4,128)}) custom-call(f32[1,32]{1,0:T(1,128)} %get-tuple-element.6.kl_ref, f32[4,576]{1,0:T(4,128)} %get-tuple-element.7.hg_ref), custom_call_target="tpu_custom_call" | custom-call | tf_op jit(solution)/shard_map/pallas_call | solution.py:369

commit v4 on v3

--- a/solution.py
+++ b/solution.py
@@ -92,48 +92,63 @@
     for d in far_first:
         send(G.at[c, chip], G.at[c, chip], a23s, a2r.at[d - 1], at(x, lax.rem(y + d, Y), c))
 
-    def along_x(slot):
-        for d in range(1, X):
-            send(G.at[c, slot], G.at[c, slot], a23s, a3r.at[d - 1], at(lax.rem(x + d, X), y, c))
-
-    along_x(chip)
+    halves, half = Y // Bc, R // 2
+    early = lax.rem(z + L, Z)
+    early_x, early_y = lax.div(early, halves), lax.rem(early, halves) * Bc
+    early_d = lax.rem(x - early_x + X, X)
+    starts = [early_y] + [lax.rem(early_y + n * Bc, Y) for n in range(1, halves)]
+
+    def group(d, h):
+        return pl.ds(lax.rem(x + X - d, X) * Y + starts[h], Bc)
+
+    def across(d, h):
+        send(G.at[c, group(d, h)], G.at[c, group(d, h)], a4s, a4r.at[d, h], partner)
+
+    def along_x(from_y):
+        h = lax.rem(lax.div(from_y, Bc) - lax.div(early_y, Bc) + halves, halves)
+        slot = x * Y + from_y
+        for d in sorted(range(1, X), key=lambda d: -min(d, X - d)):
+            send(G.at[c, slot], G.at[c, slot], a23s, a3r.at[d - 1, h], at(lax.rem(x + d, X), y, c))
+
+    along_x(y)
     for d in reversed(far_first):
-        slot = x * Y + lax.rem(y + Y - d, Y)
-        await_bytes(G.at[c, slot], a2r.at[d - 1])
-        along_x(slot)
-    for d in range(X):
-        row = pl.ds(lax.rem(x + X - d, X) * Y, Y)
-        if d:
-            await_bytes(G.at[c, row], a3r.at[d - 1])
-        send(G.at[c, row], G.at[c, row], a4s, a4r.at[d], partner)
-    for d in range(X):
-        row = pl.ds(lax.rem(x + X - d, X) * Y, Y)
-        await_bytes(G.at[1 - c, row], a4r.at[d])
-
-    half = R // 2
-    for m in range(2):
-        for core in range(2):
-
-            def arrange(b, carry, m=m, core=core):
+        from_y = lax.rem(y + Y - d, Y)
+        await_bytes(G.at[c, x * Y + from_y], a2r.at[d - 1])
+        along_x(from_y)
+    for h in range(halves):
+        across(0, h)
+
+    @pl.when(early_d != 0)
+    def _():
+        await_bytes(G.at[c, group(early_d, 0)], a3r.at[early_d - 1, 0])
+        across(early_d, 0)
+
+    def arrange(b, carry):
+        for m in range(2):
+            for core in range(2):
                 rows = [G[core, b * Bc + p, m].astype(f32) for p in range(Bc)]
                 place = pl.ds(pl.multiple_of(b * R + core * half, half), half)
                 S[m, place, :] = jnp.concatenate(rows, axis=0).astype(bf16)
-                return carry
-
-            lax.fori_loop(0, Z, arrange, 0)
-
+        return carry
+
+    await_bytes(G.at[1 - c, group(early_d, 0)], a4r.at[early_d, 0])
+    arrange(early, 0)
     for m in range(2):
         await_bytes(H.at[m], hsem.at[m])
 
+    def multiply(j, m, rows):
+        width = min(CH, VR - j * CH)
+        cols = H[m, :, j * CH : j * CH + width]
+        Pt[j, m, rows, :width] = jnp.dot(S[m, rows, :], cols, preferred_element_type=f32)
+
     for k in range(L, 0, -1):
 
         def stage(j, carry, k=k):
-            if k == L:
-                width = min(CH, VR - j * CH)
-                for m in range(2):
-                    cols = H[m, :, j * CH : j * CH + width]
-                    Pt[j, m, :, :width] = jnp.dot(S[m], cols, preferred_element_type=f32)
             for m in range(2):
+                if k == L:
+                    multiply(j, m, pl.ds(pl.multiple_of(early * R, R), R))
+                elif k == L - 1:
+                    multiply(j, m, pl.ds(0, T))
                 for s in range(2):
                     first = L if s == m else L - 1
                     if k > first:
@@ -152,7 +167,24 @@
                     send(sbuf.at[slot], rbuf.at[s, k - 1, j, m], bs, br.at[s, k - 1, j, m], beside[s])
             return carry
 
-        if k == L:
+        if k == L - 1:
+            for d in range(1, X):
+                for h in range(halves):
+
+                    @pl.when((early_d != d) if h == 0 else (early_d >= 0))
+                    def _():
+                        await_bytes(G.at[c, group(d, h)], a3r.at[d - 1, h])
+                        across(d, h)
+
+            for d in range(X):
+                for h in range(halves):
+
+                    @pl.when((early_d != d) if h == 0 else (early_d >= 0))
+                    def _():
+                        await_bytes(G.at[1 - c, group(d, h)], a4r.at[d, h])
+
+            lax.fori_loop(0, Z, arrange, 0)
+        if k >= L - 1:
             for j in range(NJ):
                 stage(j, 0)
         else:
@@ -217,22 +249,21 @@
     kl_row = jnp.sum(jnp.where(lane == natural(row), kl, 0.0), axis=0, keepdims=True)
     kl_ref[...] = kl_row[:, :R]
 
-    blocks_in_x = Y // Bc
-
-    def to_partner(slots, sources):
-        total_ = None
-        for j in range(NJ):
-            width = min(CH, VR - j * CH)
-            rows = jnp.concatenate([gbuf[t, j] for t in sources], axis=0) if len(sources) > 1 else gbuf[sources[0], j]
-            part = lax.dot_general(
-                rows[:, :width],
-                H[0, :, j * CH : j * CH + width],
-                (((1,), (1,)), ((), ())),
-                preferred_element_type=f32,
-            )
-            total_ = part if total_ is None else total_ + part
+
+    def product(j, sources):
+        width = min(CH, VR - j * CH)
+        rows = [gbuf[t, j] for t in sources]
+        rows = jnp.concatenate(rows, axis=0) if len(rows) > 1 else rows[0]
+        return lax.dot_general(
+            rows[:, :width],
+            H[0, :, j * CH : j * CH + width],
+            (((1,), (1,)), ((), ())),
+            preferred_element_type=f32,
+        )
+
+    def to_partner(slots, both):
         for n, slot in enumerate(slots):
-            hgb[slot] = total_[n * R : (n + 1) * R]
+            hgb[slot] = both[n * R : (n + 1) * R]
             theirs = pl.ds(pl.multiple_of((1 - c) * half, half), half)
             send(hgb.at[slot, theirs], ecr.at[slot], ecs, ecrs.at[slot], partner)
 
@@ -241,7 +272,7 @@
             await_bytes(ecr.at[slot], ecrs.at[slot])
             ours = pl.ds(pl.multiple_of(c * half, half), half)
             both = hgb[slot, ours] + ecr[slot]
-            tx, ty = lax.div(t, blocks_in_x), lax.rem(t, blocks_in_x) * Bc
+            tx, ty = lax.div(t, halves), lax.rem(t, halves) * Bc
             for i in range(Bc):
                 piece = both[4 * i : 4 * i + 4]
                 es[slot, i] = piece
@@ -255,8 +286,13 @@
                     send(es.at[slot, i], ey.at[tx * Y + y], eys, eyr.at[tx], at(x, ty + i, c))
 
     pending = ([0], [z])
-    to_partner(*pending)
+    to_partner([0], functools.reduce(jnp.add, [product(j, [z]) for j in range(NJ)]))
     for d in range(1, L + 1):
+        if d < L:
+            now = ([2 * d - 1, 2 * d], [lax.rem(z - d + Z, Z), lax.rem(z + d, Z)])
+        else:
+            now = ([2 * d - 1], [lax.rem(z + d, Z)])
+        both = None
         for j in range(NJ):
             for s in range(2):
                 reach = L if s == j % 2 else L - 1
@@ -266,16 +302,16 @@
                 await_bytes(gbuf.at[src, j], dr.at[s, d - 1, j])
                 if d < reach:
                     send(gbuf.at[src, j], gbuf.at[src, j], ds_, dr.at[s, d, j], beside[s])
+            if d == L:
+                both = product(j, now[1]) if both is None else both + product(j, now[1])
         if d < L:
-            now = ([2 * d - 1, 2 * d], [lax.rem(z - d + Z, Z), lax.rem(z + d, Z)])
-        else:
-            now = ([2 * d - 1], [lax.rem(z + d, Z)])
-        to_partner(*now)
+            both = functools.reduce(jnp.add, [product(j, now[1]) for j in range(NJ)])
+        to_partner(now[0], both)
         along_y(*pending)
         pending = now
     along_y(*pending)
 
-    last = lax.div(lax.rem(z + L, Z), blocks_in_x)
+    last = lax.div(lax.rem(z + L, Z), halves)
     for i in range(X):
         tx = lax.rem(last + 1 + i, X)
         await_bytes(ey.at[pl.ds(0, Y - 1)], eyr.at[tx])
@@ -345,8 +381,8 @@
                 pltpu.VMEM((X, 4, K), f32),
                 dma((2,)),
                 dma((Y - 1,)),
-                dma((X - 1,)),
-                dma((X,)),
+                dma((X - 1, Y // Bc)),
+                dma((X, Y // Bc)),
                 dma,
                 dma,
                 dma,

time: 91.5 us -> 90.4 us (0.988)
  Pallas kernels: 89.4 us -> 88.3 us
    pallas_call x1, Pallas kernels: 88 us -> 87 us  [per_device(): pl.pallas_call(functools.partial(program, (X, Y, Z, VR, CH, NJ)), out_sha...]
where the time goes in v4:
time: 90.4 us; the launch traced here: 89 us
  Pallas kernels  88.3 us (98%)
    pallas_call x1, Pallas kernels, per_device(): pl.pallas_call(functools.partial(program, (X, Y, Z, VR, CH, NJ)), out_sha...  87 us

profile of v4, /device:TPU:1, one launch (start us, length us, event | category | flops | bytes accessed | tf_op | source)
XLA Modules:
  0.0 89.0 jit_solution(647233278895520898)
XLA Ops:
  0.6 87.0 %shard_map.68 = (f32[1,32]{1,0:T(1,128)}, f32[4,576]{1,0:T(4,128)}) custom-call(bf16[4,576]{1,0:T(4,128)(2,1)} %sh_ref.1, bf16[4,576]{1,0:T(4,128)(2,1)} %th_ref.1, f32[1,256]{1,0:T(1,128)} %bitcast.6, bf16[576,2000]{1,0:T(8,128)(2,1)} %bitcast.4, bf16[576,2000]{1,0:T(8,128)(2,1)} %bitcast.5), custom_call_target="tpu_custom_call" | custom-call | tf_op jit(solution)/shard_map/pallas_call | solution.py:358
  87.6 1.3 %shard_map.69 = (f32[1,32]{1,0:T(1,128)}, f32[4,576]{1,0:T(4,128)}) custom-call(f32[1,32]{1,0:T(1,128)} %get-tuple-element.6.kl_ref, f32[4,576]{1,0:T(4,128)} %get-tuple-element.7.hg_ref), custom_call_target="tpu_custom_call" | custom-call | tf_op jit(solution)/shard_map/pallas_call | solution.py:405

commit v5 on v4

--- a/solution.py
+++ b/solution.py
@@ -168,25 +168,26 @@
             return carry
 
         if k == L - 1:
-            for d in range(1, X):
-                for h in range(halves):
-
-                    @pl.when((early_d != d) if h == 0 else (early_d >= 0))
-                    def _():
-                        await_bytes(G.at[c, group(d, h)], a3r.at[d - 1, h])
-                        across(d, h)
-
             for d in range(X):
                 for h in range(halves):
 
                     @pl.when((early_d != d) if h == 0 else (early_d >= 0))
                     def _():
                         await_bytes(G.at[1 - c, group(d, h)], a4r.at[d, h])
-
-            lax.fori_loop(0, Z, arrange, 0)
+                        arrange(lax.rem(x + X - d, X) * halves + lax.div(starts[h], Bc), 0)
+
         if k >= L - 1:
             for j in range(NJ):
                 stage(j, 0)
+                if k == L and j == (NJ - 1) // 2:
+                    for d in range(1, X):
+                        for h in range(halves):
+
+                            @pl.when((early_d != d) if h == 0 else (early_d >= 0))
+                            def _():
+                                await_bytes(G.at[c, group(d, h)], a3r.at[d - 1, h])
+                                across(d, h)
+
         else:
             lax.fori_loop(0, NJ, stage, 0)
 

time: 90.4 us -> 89.3 us (0.988)
  no operation moved by 1% of the time
where the time goes in v5:
time: 89.3 us; the launch traced here: 88.1 us
  Pallas kernels  87.5 us (98%)
    pallas_call x1, Pallas kernels, per_device(): pl.pallas_call(functools.partial(program, (X, Y, Z, VR, CH, NJ)), out_sha...  86.1 us

profile of v5, /device:TPU:1, one launch (start us, length us, event | category | flops | bytes accessed | tf_op | source)
XLA Modules:
  0.0 88.1 jit_solution(4443950124622377146)
XLA Ops:
  0.6 86.1 %shard_map.68 = (f32[1,32]{1,0:T(1,128)}, f32[4,576]{1,0:T(4,128)}) custom-call(bf16[4,576]{1,0:T(4,128)(2,1)} %sh_ref.1, bf16[4,576]{1,0:T(4,128)(2,1)} %th_ref.1, f32[1,256]{1,0:T(1,128)} %bitcast.6, bf16[576,2000]{1,0:T(8,128)(2,1)} %bitcast.4, bf16[576,2000]{1,0:T(8,128)(2,1)} %bitcast.5), custom_call_target="tpu_custom_call" | custom-call | tf_op jit(solution)/shard_map/pallas_call | solution.py:359
  86.8 1.3 %shard_map.69 = (f32[1,32]{1,0:T(1,128)}, f32[4,576]{1,0:T(4,128)}) custom-call(f32[1,32]{1,0:T(1,128)} %get-tuple-element.6.kl_ref, f32[4,576]{1,0:T(4,128)} %get-tuple-element.7.hg_ref), custom_call_target="tpu_custom_call" | custom-call | tf_op jit(solution)/shard_map/pallas_call | solution.py:406
